TPU v7x, 32 devices: a whole 2x2x4 slice. The times are simulated.
32 devices in a mesh: parts: 2 (over y), modes: 16 (over z, x, core).
Axes of the slice: x: 2, y: 2, z: 4, core: 2. Of those that a mesh axis runs over, the one named last changes fastest.
Arguments:
- stem: bfloat16 [2, 16, 64, 32, 512], P(None, 'modes', None, None, 'parts'), parts along dimension 4, may hold values from -6 to 6
- branch_one: bfloat16 [2, 1024, 1024], replicated, may hold values from -0.125 to 0.125
- branch_two: bfloat16 [2, 1024, 1024], replicated, may hold values from -0.125 to 0.125
- branch_three: bfloat16 [2, 2, 16, 512, 512], P(None, None, 'modes'), may hold values from -0.0625 to 0.0625
- leg_orders: int32 [2, 10], replicated, may hold values from 0 to 9, each once within a row
- slice_pick: int32 [32], P('parts'), parts along dimension 0, may hold values from 0 to 1
Outputs:
- contracted: bfloat16 [1024, 2, 2, 2, 256], P(('parts', 'modes')), parts along dimension 0
There are 2 independent parts, one for each index of `parts`. A program takes and returns all parts, laid end to end along the dimension named above; an argument that names none is the same for every part. Nothing has to cross between parts.
Inputs may be any that keep to these rules, and one draw needn't show every extreme that they name: `leg_orders`: each row names every input leg bit once.
All inputs are finite; a program needn't handle non-finite values.
Results may differ from a plain program's by a relative error of at most 0.008.
Values may be sent and summed in bfloat16 or wider, within the bound.
A program may use at most 128 MiB of HBM per device.

v0:
```python
import jax
import jax.numpy as jnp
from jax import lax
from jax.experimental import pallas as pl
from jax.experimental.pallas import tpu as pltpu
from jax.sharding import PartitionSpec as P

TILES = 4


def turn_columns(order, branch, out, onehot):
    width = branch.shape[1]

    @pl.when(pl.program_id(0) == 0)
    def _():
        positions = lax.broadcasted_iota(jnp.int32, (1, width), 1)
        source = jnp.zeros((1, width), jnp.int32)
        for bit in range(order.shape[0]):
            source += jnp.left_shift(jnp.right_shift(positions, bit) & 1, order[bit])
        rows = lax.broadcasted_iota(jnp.int32, (width, width), 0)
        onehot[...] = jnp.where(rows == source, 1.0, 0.0).astype(onehot.dtype)

    out[...] = jnp.dot(
        branch[...], onehot[...], preferred_element_type=jnp.float32
    ).astype(out.dtype)


def turned(branch, order, name):
    width = branch.shape[2]
    flat = branch.reshape(-1, width)
    tile = flat.shape[0] // 8
    out = pl.pallas_call(
        turn_columns,
        name=name,
        grid=(8,),
        out_shape=jax.ShapeDtypeStruct(flat.shape, flat.dtype),
        in_specs=[
            pl.BlockSpec(memory_space=pltpu.SMEM),
            pl.BlockSpec((tile, width), lambda i: (i, 0)),
        ],
        out_specs=pl.BlockSpec((tile, width), lambda i: (i, 0)),
        scratch_shapes=[pltpu.VMEM((width, width), flat.dtype)],
        compiler_params=pltpu.CompilerParams(vmem_limit_bytes=58 * 2**20),
        cost_estimate=pl.CostEstimate(
            flops=2 * flat.shape[0] * width * width,
            bytes_accessed=4 * flat.size,
            transcendentals=0,
        ),
    )(order, flat)
    return out.reshape(branch.shape)


def complex_tile(w, values):
    half = values.shape[1] // 2
    p = jnp.dot(w[0], values, preferred_element_type=jnp.float32)
    q = jnp.dot(w[1], values, preferred_element_type=jnp.float32)
    real = p[:, :half] - q[:, half:]
    imag = p[:, half:] + q[:, :half]
    return real.astype(jnp.bfloat16), imag.astype(jnp.bfloat16)


def two_branches(x_hbm, w1_hbm, w2_hbm, out, x, w1, w2, mid, sems):
    width = x.shape[0]
    half = width // 2
    tile = width // TILES
    lanes = x.shape[1] // 8
    copies = [pltpu.make_async_copy(x_hbm, x, sems.at[0])]
    for which, (source, target) in enumerate(((w1_hbm, w1), (w2_hbm, w2))):
        for i in range(TILES):
            rows = pl.ds(i * tile, tile)
            copies.append(
                pltpu.make_async_copy(
                    source.at[:, rows, :], target.at[:, rows, :], sems.at[1 + which * TILES + i]
                )
            )
    for copy in copies:
        copy.start()
    copies[0].wait()
    for i in range(TILES):
        copies[1 + i].wait()
        t, c = divmod(i * tile, half)
        parts = complex_tile(w1[:, i * tile : (i + 1) * tile, :], x[...])
        for r in range(2):
            for a in range(2):
                at = (2 * r + t) * 2 * lanes
                mid[a * half + c : a * half + c + tile, at : at + 2 * lanes] = parts[r][
                    :, a * 2 * lanes : (a + 1) * 2 * lanes
                ]
    for i in range(TILES):
        copies[1 + TILES + i].wait()
        u, c = divmod(i * tile, half)
        parts = complex_tile(w2[:, i * tile : (i + 1) * tile, :], mid[...])
        for r in range(2):
            for td in range(4):
                at = (2 * r + u) * lanes
                out[td, c : c + tile, at : at + lanes] = parts[r][:, td * lanes : (td + 1) * lanes]


def third_branch(place, wa, wb, wc, wd, values, out):
    k2 = place[0]
    k0 = place[1]
    half = values.shape[2] // 2
    p = q = None
    for w, t, d in ((wa, k2, k0), (wb, 1 - k2, k0), (wc, k2, 1 - k0), (wd, 1 - k2, 1 - k0)):
        block = values[2 * t + d]
        pp = jnp.dot(w[0], block, preferred_element_type=jnp.float32)
        qq = jnp.dot(w[1], block, preferred_element_type=jnp.float32)
        p = pp if p is None else p + pp
        q = qq if q is None else q + qq
    out[:, :half] = (p[:, :half] - q[:, half:]).astype(out.dtype)
    out[:, half:] = (p[:, half:] + q[:, :half]).astype(out.dtype)


def per_device(stem, branch_one, branch_two, branch_three, leg_orders, slice_pick):
    groups = lax.axis_size("modes")
    me = lax.axis_index("modes")
    rest = groups // 8
    entries, lanes = stem.shape[2], stem.shape[4] // 2
    k2 = (me // (2 * rest)) % 2
    quarter = me // (2 * rest)
    k0 = me % 2

    cut = stem.reshape(2, entries, 2, 2, rest, 2, 2, 2, lanes)
    cut = cut.transpose(3, 7, 4, 5, 1, 0, 2, 6, 8).reshape(groups, entries, 8 * lanes)
    pick = lax.dynamic_index_in_dim(slice_pick, me, 0, keepdims=False)
    own = lax.dynamic_index_in_dim(branch_three, pick, 0, keepdims=False)[:, 0]
    q = 2 * rest
    middle = [(q + i, 2 * q + i) for i in range(q)]
    middle += [(b, a) for a, b in middle]
    outer = [(i, i ^ q) for i in range(groups)] if q & (q - 1) == 0 else [
        (i, i + q if (i // q) % 2 == 0 else i - q) for i in range(groups)
    ]
    cores = [(i, i ^ 1) for i in range(groups)]
    crossed = lax.ppermute(own, "modes", middle)
    w1 = turned(branch_one, leg_orders[0], "turn_one")
    cut, crossed, w1, branch_two = lax.optimization_barrier((cut, crossed, w1, branch_two))
    arrived = lax.all_to_all(cut, "modes", split_axis=0, concat_axis=0, tiled=True)
    x = arrived.reshape(groups * entries, 8 * lanes)
    w2 = turned(branch_two, leg_orders[1], "turn_two")
    crossed, w2 = lax.optimization_barrier((crossed, w2))
    inner = (quarter == 1) | (quarter == 2)
    wa = jnp.where(inner, crossed, own)
    wb = lax.ppermute(wa, "modes", outer)
    wc = lax.ppermute(wa, "modes", cores)
    wd = lax.ppermute(wb, "modes", cores)

    width = w1.shape[1]
    half = width // 2
    any_spec = pl.BlockSpec(memory_space=pl.ANY)
    vmem = pl.BlockSpec(memory_space=pltpu.VMEM)
    values = pl.pallas_call(
        two_branches,
        name="two_branches",
        out_shape=jax.ShapeDtypeStruct((4, half, 4 * lanes), jnp.bfloat16),
        in_specs=[any_spec] * 3,
        out_specs=vmem,
        scratch_shapes=[
            pltpu.VMEM(x.shape, x.dtype),
            pltpu.VMEM(w1.shape, w1.dtype),
            pltpu.VMEM(w2.shape, w2.dtype),
            pltpu.VMEM((width, 8 * lanes), jnp.bfloat16),
            pltpu.SemaphoreType.DMA((1 + 2 * TILES,)),
        ],
        compiler_params=pltpu.CompilerParams(vmem_limit_bytes=58 * 2**20),
        cost_estimate=pl.CostEstimate(
            flops=8 * width * width * 8 * lanes, bytes_accessed=12 * 2**20, transcendentals=0
        ),
    )(x, w1, w2)

    out_width = own.shape[1]
    partial = pl.pallas_call(
        third_branch,
        name="third_branch",
        out_shape=jax.ShapeDtypeStruct((out_width, 4 * lanes), jnp.bfloat16),
        in_specs=[pl.BlockSpec(memory_space=pltpu.SMEM)] + [vmem] * 5,
        out_specs=vmem,
        compiler_params=pltpu.CompilerParams(vmem_limit_bytes=24 * 2**20),
        cost_estimate=pl.CostEstimate(
            flops=16 * out_width * half * 4 * lanes, bytes_accessed=7 * 2**20, transcendentals=0
        ),
    )(jnp.stack([k2, k0]).astype(jnp.int32), wa, wb, wc, wd, values)

    pieces = lax.all_to_all(partial, "modes", split_axis=0, concat_axis=0, tiled=True)
    mine = out_width // groups
    pieces = pieces.reshape(2, 2, rest, 2, mine, 2, 2, lanes).astype(jnp.float32)
    summed = jnp.sum(pieces, axis=(0, 2)).astype(jnp.bfloat16)
    return summed.transpose(2, 3, 4, 1, 0, 5).reshape(mine, 2, 2, 2, 2 * lanes)


def solution(mesh):
    in_specs = (
        P(None, "modes", None, None, "parts"),
        P(),
        P(),
        P(None, None, "modes", None, None),
        P(),
        P("parts"),
    )
    out_specs = P(("parts", "modes"), None, None, None, None)
    return jax.shard_map(
        per_device, mesh=mesh, in_specs=in_specs, out_specs=out_specs, check_vma=False
    )
```

profile of v0, /device:TPU:0, one launch (start us, length us, event | category | flops | bytes accessed | tf_op | source)
XLA Modules:
  0.0 136.7 jit_solution(2437138684387349122)
XLA Ops:
  0.0 1.4 %dynamic_slice.8 = s32[1]{0:T(128)} dynamic-slice(s32[16]{0:T(128)} %param.11, s32[]{:T(128)S(6)} %select_n.36), dynamic_slice_sizes={1} | dynamic-slice | bytes 12 | tf_op jit(solution)/shard_map/jit(dynamic_index_in_dim)/dynamic_slice | solution.py:125
  3.3 1.3 dynamic-slice_bitcast_fusion
  4.6 1.7 %collective-permute-start = (bf16[2,512,512]{2,1,0:T(8,128)(2,1)S(1)}, bf16[2,512,512]{2,1,0:T(8,128)(2,1)}, u32[]{:S(2)}, u32[]{:S(2)}) collective-permute-start(bf16[2,512,512]{2,1,0:T(8,128)(2,1)S(1)} %dynamic-slice_bitcast_fusion), channel_id=1, source_target_pairs={{4,8},{5,9},{6,10},{7,11},{8,4},{9,5},{10,6},{11,7},{20,24},{21,25... | collective-permute-start | bytes 3145736 | tf_op jit(solution)/shard_map/ppermute | solution.py:134
  6.3 0.0 copy-done.2
  6.3 2.1 %reshape.31 = bf16[2,64,2,2,2,2,2,2,128]{8,7,6,5,4,3,2,1,0:T(2,128)(2,1)} reshape(bf16[2,1,64,32,256]{4,3,2,1,0:T(8,128)(2,1)S(1)} %copy-done.2) | data formatting | bytes 4194304 | tf_op jit(solution)/shard_map/reshape | solution.py:123
  8.4 3.1 %copy.9 = bf16[2,2,2,2,64,2,2,2,128]{8,7,6,5,4,3,2,1,0:T(2,128)(2,1)S(1)} copy(bf16[2,2,2,2,64,2,2,2,128]{8,1,7,3,2,0,6,4,5:T(2,128)(2,1)} %bitcast.22) | data formatting | bytes 4194304 | tf_op jit(solution)/shard_map/transpose | solution.py:124
  11.5 0.0 copy-start.3
  11.5 2.8 %reshape.32 = bf16[16,64,1024]{2,1,0:T(8,128)(2,1)} reshape(bf16[2,2,2,2,64,2,2,2,128]{8,7,6,5,4,3,2,1,0:T(2,128)(2,1)S(1)} %copy.9) | data formatting | bytes 4194304 | tf_op jit(solution)/shard_map/reshape | solution.py:124
  14.3 0.0 copy-done.3
  14.3 0.5 slice_bitcast_fusion
  14.8 9.7 %turn_one.1 = bf16[2048,1024]{1,0:T(8,128)(2,1)} custom-call(s32[10]{0:T(128)} %get-tuple-element.18.order, bf16[2048,1024]{1,0:T(8,128)(2,1)} %bitcast.24), custom_call_target="tpu_custom_call" | custom-call | flops 4294967296 | bytes 8388608 | tf_op jit(solution)/shard_map/turn_one/pallas_call | solution.py:32
  24.5 0.0 collective-permute-done
  24.5 13.5 %all-to-all-start = ((bf16[16,64,1024]{2,1,0:T(8,128)(2,1)}), bf16[16,64,1024]{2,1,0:T(8,128)(2,1)}, u32[]{:S(2)}, u32[]{:S(2)}) async-start(bf16[16,64,1024]{2,1,0:T(8,128)(2,1)} %reshape.32), calls=%async_computation | async-start | bytes 4194304 | tf_op jit(solution)/shard_map/all_to_all | solution.py:137
  38.0 0.0 copy-start.1
  38.0 9.9 %turn_two.1 = bf16[2048,1024]{1,0:T(8,128)(2,1)} custom-call(s32[10]{0:T(128)} %get-tuple-element.17.order, bf16[2048,1024]{1,0:T(8,128)(2,1)} %bitcast.25), custom_call_target="tpu_custom_call" | custom-call | flops 4294967296 | bytes 8388608 | tf_op jit(solution)/shard_map/turn_two/pallas_call | solution.py:32
  47.9 0.1 broadcast_select_fusion.wa
  48.1 3.1 %collective-permute-start.1 = (bf16[2,512,512]{2,1,0:T(8,128)(2,1)S(1)}, bf16[2,512,512]{2,1,0:T(8,128)(2,1)S(1)}, u32[]{:S(2)}, u32[]{:S(2)}) collective-permute-start(bf16[2,512,512]{2,1,0:T(8,128)(2,1)S(1)} %broadcast_select_fusion.wa), channel_id=1, source_target_pairs={{0,4},{1,5},{2,6},{3,7},{4,0},{5,1},{6,2},{7,3},{8,12},{9,13},{10,... | collective-permute-start | bytes 3145736 | tf_op jit(solution)/shard_map/ppermute | solution.py:143
  51.2 0.0 collective-permute-start.2
  51.2 46.0 %collective-permute-done.1.wb = bf16[2,512,512]{2,1,0:T(8,128)(2,1)S(1)} collective-permute-done((bf16[2,512,512]{2,1,0:T(8,128)(2,1)S(1)}, bf16[2,512,512]{2,1,0:T(8,128)(2,1)S(1)}, u32[]{:S(2)}, u32[]{:S(2)}) %collective-permute-start.1) | collective-permute-done | bytes 1048608 | tf_op jit(solution)/shard_map/ppermute | solution.py:143
  97.2 0.0 collective-permute-start.3
  97.2 0.1 pad_add_fusion.place
  97.3 0.0 all-to-all-done
  97.3 13.4 %two_branches.1.values = bf16[4,512,512]{2,1,0:T(8,128)(2,1)} custom-call(bf16[1024,1024]{1,0:T(8,128)(2,1)} %bitcast.11.x_hbm, bf16[2,1024,1024]{2,1,0:T(8,128)(2,1)} %bitcast.26, bf16[2,1024,1024]{2,1,0:T(8,128)(2,1)} %bitcast.27), custom_call_target="tpu_custom_call" | custom-call | flops 8589934592 | bytes 12582912 | tf_op jit(solution)/shard_map/two_branches/pallas_call | solution.py:151
  110.7 0.0 collective-permute-done.2.wc
  110.7 0.0 collective-permute-done.3.wd
  110.7 1.6 %copy-done = bf16[4,512,512]{2,1,0:T(8,128)(2,1)S(1)} copy-done((bf16[4,512,512]{2,1,0:T(8,128)(2,1)S(1)}, bf16[4,512,512]{2,1,0:T(8,128)(2,1)}, u32[]{:S(2)}) %copy-start) | copy-done | bytes 2097176
  112.3 3.6 %third_branch.1 = bf16[512,512]{1,0:T(8,128)(2,1)S(1)} custom-call(s32[2]{0:T(128)S(1)} %pad_add_fusion.place, bf16[2,512,512]{2,1,0:T(8,128)(2,1)S(1)} %broadcast_select_fusion.wa, bf16[2,512,512]{2,1,0:T(8,128)(2,1)S(1)} %collective-permute-done.1.wb, bf16[2,512,512]{2,1,0:T(8,128)(2,1)S(1)} %collective-permute-done.2.wc, ...), custom_call_target="tpu_custom_call" | custom-call | flops 2147483648 | bytes 7340032 | tf_op jit(solution)/shard_map/third_branch/pallas_call | solution.py:171
  115.8 19.1 %all_to_all.14 = bf16[16,32,512]{2,1,0:T(8,128)(2,1)S(1)} all-to-all(bf16[16,32,512]{2,1,0:T(8,128)(2,1)S(1)} %bitcast.21), channel_id=1, replica_groups=mesh['parts'=2,'modes'=16] {'modes'}, dimensions={0} | all-to-all | bytes 1048576 | tf_op jit(solution)/shard_map/all_to_all | solution.py:183
  135.0 0.1 reshape.38
  135.1 0.8 reduce_sum.12
  135.9 0.1 copy.12
  136.0 0.7 reshape.40
  (3 shorter events, 0.0 us)
Async XLA Ops:
  0.0 6.3 %copy-start.2 = (bf16[2,1,64,32,256]{4,3,2,1,0:T(8,128)(2,1)S(1)}, bf16[2,1,64,32,256]{4,3,2,1,0:T(8,128)(2,1)}, u32[]{:S(2)}) copy-start(bf16[2,1,64,32,256]{4,3,2,1,0:T(8,128)(2,1)} %param.6) | copy-start | bytes 6291460
  4.6 19.9 %collective-permute-start = (bf16[2,512,512]{2,1,0:T(8,128)(2,1)S(1)}, bf16[2,512,512]{2,1,0:T(8,128)(2,1)}, u32[]{:S(2)}, u32[]{:S(2)}) collective-permute-start(bf16[2,512,512]{2,1,0:T(8,128)(2,1)S(1)} %dynamic-slice_bitcast_fusion), channel_id=1, source_target_pairs={{4,8},{5,9},{6,10},{7,11},{8,4},{9,5},{10,6},{11,7},{20,24},{21,25... | collective-permute-start | bytes 3145736 | tf_op jit(solution)/shard_map/ppermute | solution.py:134
  11.5 2.8 %copy-start.3 = (s32[2,10]{1,0:T(2,128)S(1)}, s32[2,10]{1,0:T(2,128)}, u32[]{:S(2)}) copy-start(s32[2,10]{1,0:T(2,128)} %param.10) | copy-start | bytes 244
  24.5 72.8 %all-to-all-start = ((bf16[16,64,1024]{2,1,0:T(8,128)(2,1)}), bf16[16,64,1024]{2,1,0:T(8,128)(2,1)}, u32[]{:S(2)}, u32[]{:S(2)}) async-start(bf16[16,64,1024]{2,1,0:T(8,128)(2,1)} %reshape.32), calls=%async_computation | async-start | bytes 4194304 | tf_op jit(solution)/shard_map/all_to_all | solution.py:137
  38.0 9.9 %copy-start.1 = (bf16[2,2,1,512,512]{4,3,2,1,0:T(8,128)(2,1)S(1)}, bf16[2,2,1,512,512]{4,3,2,1,0:T(8,128)(2,1)}, u32[]{:S(2)}) copy-start(bf16[2,2,1,512,512]{4,3,2,1,0:T(8,128)(2,1)} %param.9) | copy-start | bytes 6291460
  48.1 49.1 %collective-permute-start.1 = (bf16[2,512,512]{2,1,0:T(8,128)(2,1)S(1)}, bf16[2,512,512]{2,1,0:T(8,128)(2,1)S(1)}, u32[]{:S(2)}, u32[]{:S(2)}) collective-permute-start(bf16[2,512,512]{2,1,0:T(8,128)(2,1)S(1)} %broadcast_select_fusion.wa), channel_id=1, source_target_pairs={{0,4},{1,5},{2,6},{3,7},{4,0},{5,1},{6,2},{7,3},{8,12},{9,13},{10,... | collective-permute-start | bytes 3145736 | tf_op jit(solution)/shard_map/ppermute | solution.py:143
  51.2 59.5 %collective-permute-start.2 = (bf16[2,512,512]{2,1,0:T(8,128)(2,1)S(1)}, bf16[2,512,512]{2,1,0:T(8,128)(2,1)S(1)}, u32[]{:S(2)}, u32[]{:S(2)}) collective-permute-start(bf16[2,512,512]{2,1,0:T(8,128)(2,1)S(1)} %broadcast_select_fusion.wa), channel_id=1, source_target_pairs={{0,1},{1,0},{2,3},{3,2},{4,5},{5,4},{6,7},{7,6},{8,9},{9,8},{10,11... | collective-permute-start | bytes 3145736 | tf_op jit(solution)/shard_map/ppermute | solution.py:144
  97.2 13.5 %collective-permute-start.3 = (bf16[2,512,512]{2,1,0:T(8,128)(2,1)S(1)}, bf16[2,512,512]{2,1,0:T(8,128)(2,1)}, u32[]{:S(2)}, u32[]{:S(2)}) collective-permute-start(bf16[2,512,512]{2,1,0:T(8,128)(2,1)S(1)} %collective-permute-done.1.wb), channel_id=1, source_target_pairs={{0,1},{1,0},{2,3},{3,2},{4,5},{5,4},{6,7},{7,6},{8,9},{9,8},{10,11... | collective-permute-start | bytes 3145736 | tf_op jit(solution)/shard_map/ppermute | solution.py:145
  110.7 1.6 %copy-start = (bf16[4,512,512]{2,1,0:T(8,128)(2,1)S(1)}, bf16[4,512,512]{2,1,0:T(8,128)(2,1)}, u32[]{:S(2)}) copy-start(bf16[4,512,512]{2,1,0:T(8,128)(2,1)} %two_branches.1.values) | copy-start | bytes 6291460
where the time goes:
time: 137 us
  waiting for transfers between devices  46 us (34%)
  Pallas kernels  36.6 us (27%)
  blocking collectives  19.1 us (14%)
  starting transfers between devices  18.3 us (13%)
  local copies, waits for them, and re-layouts  13.7 us (10%)
  between operations  2.07 us (2%)
    ppermute x1, waiting for transfers between devices, per_device(): wb = lax.ppermute(wa, 'modes', outer)  46 us
    pallas_call x2, Pallas kernels, turned(): pl.pallas_call(turn_columns, name=name, grid=(8,), out_shape=jax.ShapeDty...  19.6 us
    all_to_all x1, blocking collectives, per_device(): lax.all_to_all(partial, 'modes', split_axis=0, concat_axis=0, tiled=True)  19.1 us
    all_to_all x1, starting transfers between devices, per_device(): lax.all_to_all(cut, 'modes', split_axis=0, concat_axis=0, tiled=True)  13.5 us
    pallas_call x1, Pallas kernels, per_device(): pl.pallas_call(two_branches, name='two_branches', out_shape=jax.ShapeDtyp...  13.4 us
    pallas_call x1, Pallas kernels, per_device(): pl.pallas_call(third_branch, name='third_branch', out_shape=jax.ShapeDtyp...  3.56 us
    ppermute x1, starting transfers between devices, per_device(): wb = lax.ppermute(wa, 'modes', outer)  3.13 us
    transpose x1, local copies, waits for them, and re-layouts, per_device(): cut.transpose(3, 7, 4, 5, 1, 0, 2, 6, 8).reshape(groups, entries, 8 * lanes)  3.07 us
  transfers between devices with their start and end apart: 5, of which 1 were waited for; matrix products, arithmetic and copies ran while one was open for 6% of the time, Pallas kernels for 24%

commit v1 on v0

--- a/solution.py
+++ b/solution.py
@@ -6,6 +6,8 @@
 from jax.sharding import PartitionSpec as P
 
 TILES = 4
+CHUNKS = 4
+MESH = pl.DeviceIdType.MESH
 
 
 def turn_columns(order, branch, out, onehot):
@@ -111,7 +113,7 @@
     out[:, half:] = (p[:, half:] + q[:, :half]).astype(out.dtype)
 
 
-def per_device(stem, branch_one, branch_two, branch_three, leg_orders, slice_pick):
+def by_columns(stem, branch_one, branch_two, branch_three, leg_orders, slice_pick):
     groups = lax.axis_size("modes")
     me = lax.axis_index("modes")
     rest = groups // 8
@@ -187,6 +189,339 @@
     return summed.transpose(2, 3, 4, 1, 0, 5).reshape(mine, 2, 2, 2, 2 * lanes)
 
 
+def spread(order, which, start, onehot):
+    rows, width = onehot.shape
+    positions = start + lax.broadcasted_iota(jnp.int32, (1, width), 1)
+    source = jnp.zeros((1, width), jnp.int32)
+    for bit in range(order.shape[1]):
+        source += jnp.left_shift(jnp.right_shift(positions, bit) & 1, order[which, bit])
+    tile = 256
+
+    @pl.loop(0, rows // tile)
+    def _(i):
+        at = i * tile + lax.broadcasted_iota(jnp.int32, (tile, width), 0)
+        onehot[pl.ds(pl.multiple_of(i * tile, tile), tile), :] = jnp.where(
+            at == source, 1.0, 0.0
+        ).astype(onehot.dtype)
+
+
+def turn(branch, onehot, w):
+    rows, width = branch.shape[1], onehot.shape[1]
+    tile = 256
+
+    @pl.loop(0, rows // tile)
+    def _(i):
+        at = pl.ds(pl.multiple_of(i * tile, tile), tile)
+        real = jnp.dot(branch[0, at, :], onehot[...], preferred_element_type=jnp.float32)
+        real = real.astype(w.dtype)
+        w[0, at, :width] = real
+        w[1, at, width:] = real
+        imag = jnp.dot(branch[1, at, :], onehot[...], preferred_element_type=jnp.float32)
+        w[0, at, width:] = (-imag).astype(w.dtype)
+        w[1, at, :width] = imag.astype(w.dtype)
+
+
+def blocks(w):
+    rows = w.shape[1] * w.shape[2]
+    real = w[0].astype(jnp.float32).reshape(rows, w.shape[3])
+    imag = w[1].astype(jnp.float32).reshape(rows, w.shape[3])
+    return jnp.concatenate(
+        [jnp.concatenate([real, -imag], axis=1), jnp.concatenate([imag, real], axis=1)], axis=0
+    ).astype(w.dtype)
+
+
+def contraction(
+    order, pick, stem, b1, b2, w3, out,
+    xin, turned_x, cut, x, raw1, raw2, onehot, w1, w2, mid, y2, raw3, own3, relay3, cross3, acc,
+    keeps, sends, gots, load_sem, x_send, x_recv, r_send, r_recv, c_send, c_recv, s_send, s_recv,
+):
+    part, me = lax.axis_index("parts"), lax.axis_index("modes")
+    n = lax.axis_size("modes")
+    half = n // 2
+    quarter = n // 4
+    within = me % half
+    top = me // half
+    second = (me // quarter) % 2
+    m_high, m_low, d = within // 4, (within // 2) % 2, within % 2
+    inner = top != second
+    f32 = jnp.float32
+    depth = (n // 2).bit_length()
+
+    def device(index):
+        return (part, index)
+
+    def flipped(width):
+        return me + width * (1 - 2 * ((me // width) % 2))
+
+    tops = stem.shape[3]
+    loads = [pltpu.make_async_copy(w3, raw3, load_sem.at[0])]
+    for i in range(tops):
+        which = (m_high + tops - 1 - i) % tops
+        loads.append(
+            pltpu.make_async_copy(stem.at[:, :, :, which], xin.at[i], load_sem.at[1 + i])
+        )
+    loads.append(pltpu.make_async_copy(b1, raw1, load_sem.at[1 + tops]))
+    loads.append(pltpu.make_async_copy(b2, raw2, load_sem.at[2 + tops]))
+    for load in loads:
+        load.start()
+    barrier = pltpu.get_barrier_semaphore()
+    for i in range(1, n):
+        pl.semaphore_signal(barrier, inc=1, device_id=device((me + i) % n), device_id_type=MESH)
+
+    chunk = raw3.shape[3] // CHUNKS
+    loads[0].wait()
+    mine = pick[me]
+    for k in range(CHUNKS):
+        value = raw3[0, :, :, k * chunk : (k + 1) * chunk, :]
+        for j in range(1, raw3.shape[0]):
+            value = jnp.where(mine == j, raw3[j, :, :, k * chunk : (k + 1) * chunk, :], value)
+        own3[k] = value
+    pl.semaphore_wait(barrier, n - 1)
+
+    across = (1 - top) * half + (1 - second) * quarter + me % quarter
+    opposite = (1 - top) * half + within
+    beside = top * half + (1 - second) * quarter + me % quarter
+
+    def to_relay(k):
+        return pltpu.make_async_remote_copy(
+            own3.at[k], relay3.at[k], r_send.at[k], r_recv.at[k],
+            device_id=device(across), device_id_type=MESH,
+        )
+
+    def to_cross(k, source, target):
+        return pltpu.make_async_remote_copy(
+            source.at[k], cross3.at[k], c_send.at[k], c_recv.at[k],
+            device_id=device(target), device_id_type=MESH,
+        )
+
+    @pl.when(inner)
+    def _():
+        for k in range(CHUNKS):
+            to_relay(k).start()
+
+    entries, lanes = stem.shape[1], stem.shape[5]
+
+    def x_copy(target, source):
+        return pltpu.make_async_remote_copy(
+            cut.at[target], x.at[:, source], x_send.at[target], x_recv.at[source],
+            device_id=device(top * half + target), device_id_type=MESH,
+        )
+
+    def piece(z, low, e):
+        return (z * 2 + low) * 2 + e
+
+    for i in range(tops):
+        loads[1 + i].wait()
+        which = (m_high + tops - 1 - i) % tops
+        for r in range(2):
+            for a in range(2):
+                for q in range(lanes // 128):
+                    tmp = turned_x.at[(a * 2 + q) % turned_x.shape[0]]
+                    tmp[...] = (
+                        xin[i, r, :, a, :, q * 128 : (q + 1) * 128]
+                        .astype(f32)
+                        .reshape(entries * 8, 128)
+                    )
+                    for row in range(8):
+                        low, b, e = row // 4, (row // 2) % 2, row % 2
+                        at = (a * 2 + b) * lanes + q * 128
+                        cut[piece(which, low, e), r, :, at : at + 128] = tmp[
+                            pl.ds(row, entries, stride=8), :
+                        ].astype(cut.dtype)
+        for low in range(2):
+            for e in range(2):
+                target = piece(which, (m_low + 1 - low) % 2, (d + 1 - e) % 2)
+                if i == tops - 1 and low == 1 and e == 1:
+                    x[:, within] = cut[within]
+                else:
+                    x_copy(target, within).start()
+
+    loads[1 + tops].wait()
+    spread(order, 0, top * w1.shape[1] // 2, onehot.at[:, : onehot.shape[1] // 2])
+    turn(raw1, onehot.at[:, : onehot.shape[1] // 2], w1)
+    loads[2 + tops].wait()
+    spread(order, 1, 0, onehot)
+    turn(raw2, onehot, w2)
+
+    for step in range(1, half):
+        source = (within + step) % half
+        x_copy(source, source).wait_recv()
+    for step in range(1, half):
+        x_copy((within + step) % half, within).wait_send()
+
+    @pl.when(inner)
+    def _():
+        for k in range(CHUNKS):
+            to_relay(k).wait()
+            to_cross(k, relay3, beside).start()
+
+    @pl.when(jnp.logical_not(inner))
+    def _():
+        for k in range(CHUNKS):
+            to_cross(k, own3, opposite).start()
+
+    legs = w1.shape[1]
+    tile = 256
+    columns = x.shape[3] // 2
+    tiles = legs // 2 // tile
+
+    @pl.loop(0, tiles)
+    def _(i):
+        for t in range(2):
+            for r in range(2):
+                rows = pl.ds(pl.multiple_of(t * (legs // 2) + i * tile, tile), tile)
+                y = jnp.dot(
+                    w1[r, rows, :], x[...].reshape(legs, 2 * columns), preferred_element_type=f32
+                ).astype(mid.dtype)
+                for a in range(2):
+                    to = pl.ds(pl.multiple_of((r * 2 + a) * (legs // 2) + i * tile, tile), tile)
+                    mid[to, t * columns : (t + 1) * columns] = y[
+                        :, a * columns : (a + 1) * columns
+                    ]
+
+    @pl.loop(0, tiles)
+    def _(i):
+        for u in range(2):
+            for r in range(2):
+                rows = pl.ds(pl.multiple_of(u * (legs // 2) + i * tile, tile), tile)
+                y = jnp.dot(w2[r, rows, :], mid[...], preferred_element_type=f32).astype(y2.dtype)
+                to = pl.ds(pl.multiple_of(i * tile, tile), tile)
+                for t in range(2):
+                    y2[(t + top) % 2, r, to, u * columns : (u + 1) * columns] = y[
+                        :, t * columns : (t + 1) * columns
+                    ]
+
+    def applied(w, t):
+        return jnp.dot(
+            blocks(w), y2[t].reshape(legs, 2 * columns), preferred_element_type=f32
+        )
+
+    @pl.loop(0, CHUNKS)
+    def _(k):
+        acc[k] = applied(own3.at[k], 0)
+
+    def exchange(stage, k):
+        return pltpu.make_async_remote_copy(
+            sends[stage].at[k], gots[stage].at[k], s_send.at[stage, k], s_recv.at[stage, k],
+            device_id=device(flipped(1 << stage)), device_id_type=MESH,
+        )
+
+    def split(stage, k, total):
+        bit = (me // (1 << stage)) % 2
+        pairs = total.reshape(2, total.shape[1] // 2, 2, chunk, 2 * columns)
+        keeps[stage][k] = jnp.where(bit == 0, pairs[:, :, 0], pairs[:, :, 1])
+        sends[stage][k] = jnp.where(bit == 0, pairs[:, :, 1], pairs[:, :, 0]).astype(
+            sends[stage].dtype
+        )
+        exchange(stage, k).start()
+
+    def joined(stage, k):
+        exchange(stage, k).wait_recv()
+        return keeps[stage][k] + gots[stage][k].astype(f32)
+
+    for step in range(CHUNKS + depth):
+        for stage in range(depth, 0, -1):
+            k = step - stage
+            if 0 <= k < CHUNKS:
+                total = joined(stage - 1, k)
+                if stage < depth:
+                    split(stage, k, total)
+                else:
+                    out[:, k * chunk : (k + 1) * chunk, :] = total[:, 0].astype(out.dtype)
+        if step < CHUNKS:
+            to_cross(step, own3, opposite).wait_recv()
+            total = acc[step] + applied(cross3.at[step], 1)
+            split(0, step, total.reshape(2, n, chunk, 2 * columns))
+
+    @pl.when(inner)
+    def _():
+        for k in range(CHUNKS):
+            to_cross(k, relay3, beside).wait_send()
+
+    @pl.when(jnp.logical_not(inner))
+    def _():
+        for k in range(CHUNKS):
+            to_cross(k, own3, opposite).wait_send()
+
+    for stage in range(depth):
+        for k in range(CHUNKS):
+            exchange(stage, k).wait_send()
+
+
+def by_halves(stem, branch_one, branch_two, branch_three, leg_orders, slice_pick):
+    n = lax.axis_size("modes")
+    entries, heads, lanes = stem.shape[2], stem.shape[3], stem.shape[4]
+    slices, out_width, depth3 = branch_three.shape[0], branch_three.shape[3], branch_three.shape[4]
+    legs = branch_one.shape[1]
+    mine, tops = out_width // n, n // 8
+    chunk = mine // CHUNKS
+    stages = (n // 2).bit_length()
+    cut = stem.reshape(2, entries, 2, tops, 8, lanes)
+    third = branch_three.reshape(slices, 2, n, mine, depth3)
+    bf16, f32 = jnp.bfloat16, jnp.float32
+    smem = pl.BlockSpec(memory_space=pltpu.SMEM)
+    anyspace = pl.BlockSpec(memory_space=pl.ANY)
+    dma = pltpu.SemaphoreType.DMA
+
+    def halving(dtype):
+        return [
+            pltpu.VMEM((CHUNKS, 2, n >> (s + 1), chunk, 4 * lanes), dtype) for s in range(stages)
+        ]
+
+    out = pl.pallas_call(
+        contraction,
+        name="contraction",
+        out_shape=jax.ShapeDtypeStruct((2, mine, 4 * lanes), bf16),
+        in_specs=[smem, smem] + [anyspace] * 4,
+        out_specs=pl.BlockSpec(memory_space=pltpu.VMEM),
+        scratch_shapes=[
+            pltpu.VMEM((tops, 2, entries, 2, 8, lanes), bf16),
+            pltpu.VMEM((4, entries * 8, 128), f32),
+            pltpu.VMEM((n // 2, 2, entries, 4 * lanes), bf16),
+            pltpu.VMEM((2, n // 2, entries, 4 * lanes), bf16),
+            pltpu.VMEM(branch_one.shape, bf16),
+            pltpu.VMEM(branch_two.shape, bf16),
+            pltpu.VMEM((legs, legs), bf16),
+            pltpu.VMEM((2, legs, legs), bf16),
+            pltpu.VMEM((2, legs, 2 * legs), bf16),
+            pltpu.VMEM((2 * legs, 4 * lanes), bf16),
+            pltpu.VMEM((2, 2, legs // 2, 4 * lanes), bf16),
+            pltpu.VMEM(third.shape, bf16),
+            pltpu.VMEM((CHUNKS, 2, n, chunk, depth3), bf16),
+            pltpu.VMEM((CHUNKS, 2, n, chunk, depth3), bf16),
+            pltpu.VMEM((CHUNKS, 2, n, chunk, depth3), bf16),
+            pltpu.VMEM((CHUNKS, 2 * n * chunk, 4 * lanes), f32),
+            halving(f32),
+            halving(bf16),
+            halving(bf16),
+            dma((3 + tops,)),
+            dma((n // 2,)),
+            dma((n // 2,)),
+            dma((CHUNKS,)),
+            dma((CHUNKS,)),
+            dma((CHUNKS,)),
+            dma((CHUNKS,)),
+            dma((stages, CHUNKS)),
+            dma((stages, CHUNKS)),
+        ],
+        compiler_params=pltpu.CompilerParams(
+            collective_id=0, has_side_effects=True, vmem_limit_bytes=62 * 2**20
+        ),
+    )(leg_orders, slice_pick, cut, branch_one, branch_two, third)
+    return out.reshape(2, mine, 2, 2, lanes).transpose(1, 0, 2, 3, 4)
+
+
+def per_device(stem, branch_one, branch_two, branch_three, leg_orders, slice_pick):
+    groups = lax.axis_size("modes")
+    whole_tiles = (
+        groups & (groups - 1) == 0
+        and stem.shape[2] % 16 == 0
+        and branch_three.shape[3] % (groups * CHUNKS * 8) == 0
+    )
+    program = by_halves if whole_tiles else by_columns
+    return program(stem, branch_one, branch_two, branch_three, leg_orders, slice_pick)
+
+
 def solution(mesh):
     in_specs = (
         P(None, "modes", None, None, "parts"),

time: 137 us -> 78.6 us (0.57)
  waiting for transfers between devices: 46 us -> 0 us
  Pallas kernels: 36.6 us -> 76.7 us
  blocking collectives: 19.1 us -> 0 us
  starting transfers between devices: 18.3 us -> 0 us
  local copies, waits for them, and re-layouts: 13.7 us -> 1.73 us
  between operations: 2.07 us -> 0.01 us
    ppermute x4 -> x0, waiting for transfers between devices: 46 us -> none  [the longest x1 46 us: per_device(): wb = lax.ppermute(wa, 'modes', outer)]
    pallas_call x4 -> x1, Pallas kernels: 36.6 us -> 76.7 us  [by_halves(): pl.pallas_call(contraction, name='contraction', out_shape=jax.ShapeDtypeS...]
    all_to_all x1 -> x0, blocking collectives: 19.1 us -> none  [per_device(): lax.all_to_all(partial, 'modes', split_axis=0, concat_axis=0, tiled=True)]
    all_to_all x1 -> x0, starting transfers between devices: 13.5 us -> none  [per_device(): lax.all_to_all(cut, 'modes', split_axis=0, concat_axis=0, tiled=True)]
    ppermute x4 -> x0, starting transfers between devices: 4.83 us -> none  [the longest x1 3.13 us: per_device(): wb = lax.ppermute(wa, 'modes', outer)]
    reshape x5 -> x2, local copies, waits for them, and re-layouts: 5.84 us -> 1.73 us  [by_halves(): return out.reshape(2, mine, 2, 2, lanes).transpose(1, 0, 2, 3, 4)]
    transpose x1 -> x0, local copies, waits for them, and re-layouts: 3.07 us -> none  [per_device(): cut.transpose(3, 7, 4, 5, 1, 0, 2, 6, 8).reshape(groups, entries, 8 * lanes)]
    squeeze x2 -> x0, local copies, waits for them, and re-layouts: 1.82 us -> none  [the longest x1 1.3 us: per_device(): own = lax.dynamic_index_in_dim(branch_three, pick, 0, keepdims=False)[:, 0]]
  transfers between devices with their start and end apart: 5 -> 0, of which waited for: 1 -> 0; matrix products, arithmetic and copies ran while one was open for 6% -> 0% of each run, Pallas kernels for 24% -> 0%
where the time goes in v1:
time: 78.6 us; the launch traced here: 78.4 us
  Pallas kernels  76.7 us (98%)
  local copies, waits for them, and re-layouts  1.73 us (2%)
    pallas_call x1, Pallas kernels, by_halves(): pl.pallas_call(contraction, name='contraction', out_shape=jax.ShapeDtypeS...  76.7 us
    reshape x2, local copies, waits for them, and re-layouts, by_halves(): return out.reshape(2, mine, 2, 2, lanes).transpose(1, 0, 2, 3, 4)  1.73 us

profile of v1, /device:TPU:0, one launch (start us, length us, event | category | flops | bytes accessed | tf_op | source)
XLA Modules:
  0.0 78.4 jit_solution(1547138364342242319)
XLA Ops:
  0.0 76.7 %contraction.1 = bf16[2,32,1024]{2,1,0:T(8,128)(2,1)} custom-call(s32[2,10]{1,0:T(2,128)} %order.1, s32[16]{0:T(128)} %pick.1, bf16[2,64,2,2,8,256]{5,4,3,2,1,0:T(8,128)(2,1)} %bitcast.5, bf16[2,1024,1024]{2,1,0:T(8,128)(2,1)} %b1.1, bf16[2,1024,1024]{2,1,0:T(8,128)(2,1)} %b2.1, bf16[2,2,16,32,512]{4,3,2,1,0:T(8,128)(2,1)} %bitcast.6), custom_call_target="tpu_custom_call" | custom-call | tf_op jit(solution)/shard_map/contraction/pallas_call | solution.py:471
  76.7 1.0 %reshape.11 = bf16[2,32,2,2,256]{4,3,2,1,0:T(2,128)(2,1)S(1)} reshape(bf16[2,32,1024]{2,1,0:T(8,128)(2,1)} %contraction.1) | data formatting | bytes 262144 | tf_op jit(solution)/shard_map/reshape | solution.py:511
  77.6 0.7 copy.9

commit v2 on v1

--- a/solution.py
+++ b/solution.py
@@ -205,20 +205,58 @@
         ).astype(onehot.dtype)
 
 
-def turn(branch, onehot, w):
-    rows, width = branch.shape[1], onehot.shape[1]
-    tile = 256
+def turn_first(branch, onehot, w1):
+    rows, tile = branch.shape[1], 256
+    for t in range(2):
+
+        @pl.loop(0, rows // 2 // tile)
+        def _(i):
+            to = pl.ds(pl.multiple_of(i * tile, tile), tile)
+            at = pl.ds(pl.multiple_of(t * (rows // 2) + i * tile, tile), tile)
+            for r in range(2):
+                w1[t, r, to, :] = jnp.dot(
+                    branch[r, at, :], onehot[...], preferred_element_type=jnp.float32
+                ).astype(w1.dtype)
+
+
+def turn_second(branch, onehot, w2):
+    rows, tile = branch.shape[1], 256
+    half = rows // 2
 
     @pl.loop(0, rows // tile)
     def _(i):
         at = pl.ds(pl.multiple_of(i * tile, tile), tile)
         real = jnp.dot(branch[0, at, :], onehot[...], preferred_element_type=jnp.float32)
-        real = real.astype(w.dtype)
-        w[0, at, :width] = real
-        w[1, at, width:] = real
+        real = real.astype(w2.dtype)
+        for a in range(2):
+            w2[0, a, at, :half] = real[:, a * half : (a + 1) * half]
+            w2[1, a, at, half:] = real[:, a * half : (a + 1) * half]
         imag = jnp.dot(branch[1, at, :], onehot[...], preferred_element_type=jnp.float32)
-        w[0, at, width:] = (-imag).astype(w.dtype)
-        w[1, at, :width] = imag.astype(w.dtype)
+        imag = imag.astype(w2.dtype)
+        for a in range(2):
+            w2[0, a, at, half:] = -imag[:, a * half : (a + 1) * half]
+            w2[1, a, at, :half] = imag[:, a * half : (a + 1) * half]
+
+
+def joined_branches(w1, w2, w21):
+    rows, tile = w2.shape[2], 256
+    legs = w1.shape[3]
+
+    @pl.loop(0, rows // tile)
+    def _(i):
+        at = pl.ds(pl.multiple_of(i * tile, tile), tile)
+        for t in range(2):
+            first = w1[t].reshape(2 * w1.shape[2], legs)
+            for a in range(2):
+                lo, hi = a * legs, (2 + a) * legs
+                real = jnp.dot(w2[0, a, at, :], first, preferred_element_type=jnp.float32)
+                real = real.astype(w21.dtype)
+                w21[t, 0, at, lo : lo + legs] = real
+                w21[t, 1, at, hi : hi + legs] = real
+                imag = jnp.dot(w2[1, a, at, :], first, preferred_element_type=jnp.float32)
+                imag = imag.astype(w21.dtype)
+                w21[t, 0, at, hi : hi + legs] = -imag
+                w21[t, 1, at, lo : lo + legs] = imag
 
 
 def blocks(w):
@@ -232,7 +270,7 @@
 
 def contraction(
     order, pick, stem, b1, b2, w3, out,
-    xin, turned_x, cut, x, raw1, raw2, onehot, w1, w2, mid, y2, raw3, own3, relay3, cross3, acc,
+    xin, turned_x, cut, x, raw1, raw2, onehot, w1, w2, w21, y2, raw3, own3, relay3, cross3, acc,
     keeps, sends, gots, load_sem, x_send, x_recv, r_send, r_recv, c_send, c_recv, s_send, s_recv,
 ):
     part, me = lax.axis_index("parts"), lax.axis_index("modes")
@@ -265,8 +303,12 @@
     for load in loads:
         load.start()
     barrier = pltpu.get_barrier_semaphore()
-    for i in range(1, n):
-        pl.semaphore_signal(barrier, inc=1, device_id=device((me + i) % n), device_id_type=MESH)
+    across = (1 - top) * half + (1 - second) * quarter + me % quarter
+    opposite = (1 - top) * half + within
+    beside = top * half + (1 - second) * quarter + me % quarter
+    peers = [top * half + (within + i) % half for i in range(1, half)] + [across, opposite]
+    for peer in peers:
+        pl.semaphore_signal(barrier, inc=1, device_id=device(peer), device_id_type=MESH)
 
     chunk = raw3.shape[3] // CHUNKS
     loads[0].wait()
@@ -276,11 +318,6 @@
         for j in range(1, raw3.shape[0]):
             value = jnp.where(mine == j, raw3[j, :, :, k * chunk : (k + 1) * chunk, :], value)
         own3[k] = value
-    pl.semaphore_wait(barrier, n - 1)
-
-    across = (1 - top) * half + (1 - second) * quarter + me % quarter
-    opposite = (1 - top) * half + within
-    beside = top * half + (1 - second) * quarter + me % quarter
 
     def to_relay(k):
         return pltpu.make_async_remote_copy(
@@ -294,16 +331,11 @@
             device_id=device(target), device_id_type=MESH,
         )
 
-    @pl.when(inner)
-    def _():
-        for k in range(CHUNKS):
-            to_relay(k).start()
-
     entries, lanes = stem.shape[1], stem.shape[5]
 
     def x_copy(target, source):
         return pltpu.make_async_remote_copy(
-            cut.at[target], x.at[:, source], x_send.at[target], x_recv.at[source],
+            cut.at[target], x.at[:, :, source], x_send.at[target], x_recv.at[source],
             device_id=device(top * half + target), device_id_type=MESH,
         )
 
@@ -324,28 +356,35 @@
                     )
                     for row in range(8):
                         low, b, e = row // 4, (row // 2) % 2, row % 2
-                        at = (a * 2 + b) * lanes + q * 128
-                        cut[piece(which, low, e), r, :, at : at + 128] = tmp[
+                        at = b * lanes + q * 128
+                        cut[piece(which, low, e), r, a, :, at : at + 128] = tmp[
                             pl.ds(row, entries, stride=8), :
                         ].astype(cut.dtype)
+    pl.semaphore_wait(barrier, len(peers))
+
+    @pl.when(inner)
+    def _():
+        for k in range(CHUNKS):
+            to_relay(k).start()
+
+    for i in range(tops):
+        which = (m_high + tops - 1 - i) % tops
         for low in range(2):
             for e in range(2):
-                target = piece(which, (m_low + 1 - low) % 2, (d + 1 - e) % 2)
-                if i == tops - 1 and low == 1 and e == 1:
-                    x[:, within] = cut[within]
-                else:
+                if i < tops - 1 or low == 0 or e == 0:
+                    target = piece(which, (m_low + 1 - low) % 2, (d + 1 - e) % 2)
                     x_copy(target, within).start()
+    x[:, :, within] = cut[within]
 
     loads[1 + tops].wait()
-    spread(order, 0, top * w1.shape[1] // 2, onehot.at[:, : onehot.shape[1] // 2])
-    turn(raw1, onehot.at[:, : onehot.shape[1] // 2], w1)
+    legs = w1.shape[3]
+    spread(order, 0, top * legs, onehot.at[:, :legs])
+    turn_first(raw1, onehot.at[:, :legs], w1)
     loads[2 + tops].wait()
     spread(order, 1, 0, onehot)
-    turn(raw2, onehot, w2)
-
-    for step in range(1, half):
-        source = (within + step) % half
-        x_copy(source, source).wait_recv()
+    turn_second(raw2, onehot, w2)
+    joined_branches(w1, w2, w21)
+
     for step in range(1, half):
         x_copy((within + step) % half, within).wait_send()
 
@@ -360,78 +399,77 @@
         for k in range(CHUNKS):
             to_cross(k, own3, opposite).start()
 
-    legs = w1.shape[1]
-    tile = 256
-    columns = x.shape[3] // 2
-    tiles = legs // 2 // tile
-
-    @pl.loop(0, tiles)
+    for step in range(1, half):
+        source = (within + step) % half
+        x_copy(source, source).wait_recv()
+
+    tile, columns = 256, x.shape[4]
+
+    @pl.loop(0, legs // tile)
     def _(i):
-        for t in range(2):
-            for r in range(2):
-                rows = pl.ds(pl.multiple_of(t * (legs // 2) + i * tile, tile), tile)
-                y = jnp.dot(
-                    w1[r, rows, :], x[...].reshape(legs, 2 * columns), preferred_element_type=f32
-                ).astype(mid.dtype)
-                for a in range(2):
-                    to = pl.ds(pl.multiple_of((r * 2 + a) * (legs // 2) + i * tile, tile), tile)
-                    mid[to, t * columns : (t + 1) * columns] = y[
-                        :, a * columns : (a + 1) * columns
-                    ]
-
-    @pl.loop(0, tiles)
-    def _(i):
+        values = x[...].reshape(4 * legs, columns)
         for u in range(2):
-            for r in range(2):
-                rows = pl.ds(pl.multiple_of(u * (legs // 2) + i * tile, tile), tile)
-                y = jnp.dot(w2[r, rows, :], mid[...], preferred_element_type=f32).astype(y2.dtype)
-                to = pl.ds(pl.multiple_of(i * tile, tile), tile)
-                for t in range(2):
-                    y2[(t + top) % 2, r, to, u * columns : (u + 1) * columns] = y[
-                        :, t * columns : (t + 1) * columns
-                    ]
+            rows = pl.ds(pl.multiple_of(u * legs + i * tile, tile), tile)
+            to = pl.ds(pl.multiple_of(i * tile, tile), tile)
+            for t in range(2):
+                for r in range(2):
+                    y2[(t + top) % 2, r, to, u * columns : (u + 1) * columns] = jnp.dot(
+                        w21[t, r, rows, :], values, preferred_element_type=f32
+                    ).astype(y2.dtype)
 
     def applied(w, t):
         return jnp.dot(
-            blocks(w), y2[t].reshape(legs, 2 * columns), preferred_element_type=f32
-        )
-
-    @pl.loop(0, CHUNKS)
-    def _(k):
-        acc[k] = applied(own3.at[k], 0)
-
-    def exchange(stage, k):
+            blocks(w), y2[t].reshape(2 * legs, 2 * columns), preferred_element_type=f32
+        )
+
+    widths = [1 << s for s in range(depth)]
+    orders = [widths, widths[:1] + widths[1:-1][::-1] + widths[-1:]]
+
+    def exchange(u, stage, k):
         return pltpu.make_async_remote_copy(
-            sends[stage].at[k], gots[stage].at[k], s_send.at[stage, k], s_recv.at[stage, k],
-            device_id=device(flipped(1 << stage)), device_id_type=MESH,
-        )
-
-    def split(stage, k, total):
-        bit = (me // (1 << stage)) % 2
-        pairs = total.reshape(2, total.shape[1] // 2, 2, chunk, 2 * columns)
-        keeps[stage][k] = jnp.where(bit == 0, pairs[:, :, 0], pairs[:, :, 1])
-        sends[stage][k] = jnp.where(bit == 0, pairs[:, :, 1], pairs[:, :, 0]).astype(
+            sends[stage].at[u, k], gots[stage].at[u, k],
+            s_send.at[u, stage, k], s_recv.at[u, stage, k],
+            device_id=device(flipped(orders[u][stage])), device_id_type=MESH,
+        )
+
+    def split(u, stage, k, total):
+        width = orders[u][stage]
+        left = sorted(orders[u][stage:], reverse=True)
+        axis = 1 + left.index(width)
+        pairs = total.reshape((2,) + (2,) * len(left) + (chunk, columns))
+        pick_of = (slice(None),) * axis
+        zero, one = pairs[pick_of + (0,)], pairs[pick_of + (1,)]
+        bit = (me // width) % 2
+        shape = keeps[stage].shape[2:]
+        keeps[stage][u, k] = jnp.where(bit == 0, zero, one).reshape(shape)
+        sends[stage][u, k] = jnp.where(bit == 0, one, zero).reshape(shape).astype(
             sends[stage].dtype
         )
-        exchange(stage, k).start()
-
-    def joined(stage, k):
-        exchange(stage, k).wait_recv()
-        return keeps[stage][k] + gots[stage][k].astype(f32)
+        exchange(u, stage, k).start()
+
+    def advance(stage, k):
+        for u in range(2):
+            exchange(u, stage - 1, k).wait_recv()
+            total = keeps[stage - 1][u, k] + gots[stage - 1][u, k].astype(f32)
+            if stage < depth:
+                split(u, stage, k, total)
+            else:
+                out[:, k * chunk : (k + 1) * chunk, u * columns : (u + 1) * columns] = total[
+                    :, 0
+                ].astype(out.dtype)
 
     for step in range(CHUNKS + depth):
+        if step < CHUNKS:
+            acc[...] = applied(own3.at[step], 0)
+            to_cross(step, own3, opposite).wait_recv()
+            total = acc[...] + applied(cross3.at[step], 1)
+            for u in range(2):
+                part_of = total[:, u * columns : (u + 1) * columns]
+                split(u, 0, step, part_of.reshape(2, n, chunk, columns))
         for stage in range(depth, 0, -1):
-            k = step - stage
+            k = step - stage + 1
             if 0 <= k < CHUNKS:
-                total = joined(stage - 1, k)
-                if stage < depth:
-                    split(stage, k, total)
-                else:
-                    out[:, k * chunk : (k + 1) * chunk, :] = total[:, 0].astype(out.dtype)
-        if step < CHUNKS:
-            to_cross(step, own3, opposite).wait_recv()
-            total = acc[step] + applied(cross3.at[step], 1)
-            split(0, step, total.reshape(2, n, chunk, 2 * columns))
+                advance(stage, k)
 
     @pl.when(inner)
     def _():
@@ -445,7 +483,8 @@
 
     for stage in range(depth):
         for k in range(CHUNKS):
-            exchange(stage, k).wait_send()
+            for u in range(2):
+                exchange(u, stage, k).wait_send()
 
 
 def by_halves(stem, branch_one, branch_two, branch_three, leg_orders, slice_pick):
@@ -465,7 +504,8 @@
 
     def halving(dtype):
         return [
-            pltpu.VMEM((CHUNKS, 2, n >> (s + 1), chunk, 4 * lanes), dtype) for s in range(stages)
+            pltpu.VMEM((2, CHUNKS, 2, n >> (s + 1), chunk, 2 * lanes), dtype)
+            for s in range(stages)
         ]
 
     out = pl.pallas_call(
@@ -477,20 +517,20 @@
         scratch_shapes=[
             pltpu.VMEM((tops, 2, entries, 2, 8, lanes), bf16),
             pltpu.VMEM((4, entries * 8, 128), f32),
-            pltpu.VMEM((n // 2, 2, entries, 4 * lanes), bf16),
-            pltpu.VMEM((2, n // 2, entries, 4 * lanes), bf16),
+            pltpu.VMEM((n // 2, 2, 2, entries, 2 * lanes), bf16),
+            pltpu.VMEM((2, 2, n // 2, entries, 2 * lanes), bf16),
             pltpu.VMEM(branch_one.shape, bf16),
             pltpu.VMEM(branch_two.shape, bf16),
             pltpu.VMEM((legs, legs), bf16),
-            pltpu.VMEM((2, legs, legs), bf16),
-            pltpu.VMEM((2, legs, 2 * legs), bf16),
-            pltpu.VMEM((2 * legs, 4 * lanes), bf16),
+            pltpu.VMEM((2, 2, legs // 2, legs // 2), bf16),
+            pltpu.VMEM((2, 2, legs, legs), bf16),
+            pltpu.VMEM((2, 2, legs, 2 * legs), bf16),
             pltpu.VMEM((2, 2, legs // 2, 4 * lanes), bf16),
             pltpu.VMEM(third.shape, bf16),
             pltpu.VMEM((CHUNKS, 2, n, chunk, depth3), bf16),
             pltpu.VMEM((CHUNKS, 2, n, chunk, depth3), bf16),
             pltpu.VMEM((CHUNKS, 2, n, chunk, depth3), bf16),
-            pltpu.VMEM((CHUNKS, 2 * n * chunk, 4 * lanes), f32),
+            pltpu.VMEM((2 * n * chunk, 4 * lanes), f32),
             halving(f32),
             halving(bf16),
             halving(bf16),
@@ -501,8 +541,8 @@
             dma((CHUNKS,)),
             dma((CHUNKS,)),
             dma((CHUNKS,)),
-            dma((stages, CHUNKS)),
-            dma((stages, CHUNKS)),
+            dma((2, stages, CHUNKS)),
+            dma((2, stages, CHUNKS)),
         ],
         compiler_params=pltpu.CompilerParams(
             collective_id=0, has_side_effects=True, vmem_limit_bytes=62 * 2**20

time: 78.6 us -> 77.5 us (0.986)
  Pallas kernels: 76.7 us -> 75.6 us
    pallas_call x1, Pallas kernels: 76.7 us -> 75.6 us  [by_halves(): pl.pallas_call(contraction, name='contraction', out_shape=jax.ShapeDtypeS...]
where the time goes in v2:
time: 77.5 us; the launch traced here: 77.3 us
  Pallas kernels  75.6 us (98%)
  local copies, waits for them, and re-layouts  1.73 us (2%)
    pallas_call x1, Pallas kernels, by_halves(): pl.pallas_call(contraction, name='contraction', out_shape=jax.ShapeDtypeS...  75.6 us
    reshape x2, local copies, waits for them, and re-layouts, by_halves(): return out.reshape(2, mine, 2, 2, lanes).transpose(1, 0, 2, 3, 4)  1.73 us

profile of v2, /device:TPU:0, one launch (start us, length us, event | category | flops | bytes accessed | tf_op | source)
XLA Modules:
  0.0 77.3 jit_solution(4074019849845486187)
XLA Ops:
  0.0 75.6 %contraction.1 = bf16[2,32,1024]{2,1,0:T(8,128)(2,1)} custom-call(s32[2,10]{1,0:T(2,128)} %order.1, s32[16]{0:T(128)} %pick.1, bf16[2,64,2,2,8,256]{5,4,3,2,1,0:T(8,128)(2,1)} %bitcast.5, bf16[2,1024,1024]{2,1,0:T(8,128)(2,1)} %b1.1, bf16[2,1024,1024]{2,1,0:T(8,128)(2,1)} %b2.1, bf16[2,2,16,32,512]{4,3,2,1,0:T(8,128)(2,1)} %bitcast.6), custom_call_target="tpu_custom_call" | custom-call | tf_op jit(solution)/shard_map/contraction/pallas_call | solution.py:511
  75.6 1.0 %reshape.11 = bf16[2,32,2,2,256]{4,3,2,1,0:T(2,128)(2,1)S(1)} reshape(bf16[2,32,1024]{2,1,0:T(8,128)(2,1)} %contraction.1) | data formatting | bytes 262144 | tf_op jit(solution)/shard_map/reshape | solution.py:551
  76.6 0.7 copy.9

commit v3 on v2

--- a/solution.py
+++ b/solution.py
@@ -325,11 +325,22 @@
             device_id=device(across), device_id_type=MESH,
         )
 
-    def to_cross(k, source, target):
+    def to_cross(k, r, source, target):
         return pltpu.make_async_remote_copy(
-            source.at[k], cross3.at[k], c_send.at[k], c_recv.at[k],
+            source.at[k, r], cross3.at[k, r], c_send.at[k, r], c_recv.at[k, r],
             device_id=device(target), device_id_type=MESH,
         )
+
+    def send_third(k, r):
+        @pl.when(inner)
+        def _():
+            if r == 0:
+                to_relay(k).wait()
+            to_cross(k, r, relay3, beside).start()
+
+        @pl.when(jnp.logical_not(inner))
+        def _():
+            to_cross(k, r, own3, opposite).start()
 
     entries, lanes = stem.shape[1], stem.shape[5]
 
@@ -388,16 +399,9 @@
     for step in range(1, half):
         x_copy((within + step) % half, within).wait_send()
 
-    @pl.when(inner)
-    def _():
-        for k in range(CHUNKS):
-            to_relay(k).wait()
-            to_cross(k, relay3, beside).start()
-
-    @pl.when(jnp.logical_not(inner))
-    def _():
-        for k in range(CHUNKS):
-            to_cross(k, own3, opposite).start()
+    ahead = [(k, r) for k in range(CHUNKS) for r in range(2)]
+    for _ in range(4):
+        send_third(*ahead.pop(0))
 
     for step in range(1, half):
         source = (within + step) % half
@@ -423,18 +427,21 @@
         )
 
     widths = [1 << s for s in range(depth)]
-    orders = [widths, widths[:1] + widths[1:-1][::-1] + widths[-1:]]
+    swapped = widths[:1] + widths[1:-1][::-1] + widths[-1:]
+
+    def order_of(u, k):
+        return widths
 
     def exchange(u, stage, k):
         return pltpu.make_async_remote_copy(
             sends[stage].at[u, k], gots[stage].at[u, k],
             s_send.at[u, stage, k], s_recv.at[u, stage, k],
-            device_id=device(flipped(orders[u][stage])), device_id_type=MESH,
+            device_id=device(flipped(order_of(u, k)[stage])), device_id_type=MESH,
         )
 
     def split(u, stage, k, total):
-        width = orders[u][stage]
-        left = sorted(orders[u][stage:], reverse=True)
+        width = order_of(u, k)[stage]
+        left = sorted(order_of(u, k)[stage:], reverse=True)
         axis = 1 + left.index(width)
         pairs = total.reshape((2,) + (2,) * len(left) + (chunk, columns))
         pick_of = (slice(None),) * axis
@@ -461,11 +468,16 @@
     for step in range(CHUNKS + depth):
         if step < CHUNKS:
             acc[...] = applied(own3.at[step], 0)
-            to_cross(step, own3, opposite).wait_recv()
+            for r in range(2):
+                to_cross(step, r, own3, opposite).wait_recv()
+            if ahead:
+                send_third(*ahead.pop(0))
             total = acc[...] + applied(cross3.at[step], 1)
             for u in range(2):
                 part_of = total[:, u * columns : (u + 1) * columns]
                 split(u, 0, step, part_of.reshape(2, n, chunk, columns))
+            if ahead:
+                send_third(*ahead.pop(0))
         for stage in range(depth, 0, -1):
             k = step - stage + 1
             if 0 <= k < CHUNKS:
@@ -474,12 +486,14 @@
     @pl.when(inner)
     def _():
         for k in range(CHUNKS):
-            to_cross(k, relay3, beside).wait_send()
+            for r in range(2):
+                to_cross(k, r, relay3, beside).wait_send()
 
     @pl.when(jnp.logical_not(inner))
     def _():
         for k in range(CHUNKS):
-            to_cross(k, own3, opposite).wait_send()
+            for r in range(2):
+                to_cross(k, r, own3, opposite).wait_send()
 
     for stage in range(depth):
         for k in range(CHUNKS):
@@ -539,8 +553,8 @@
             dma((n // 2,)),
             dma((CHUNKS,)),
             dma((CHUNKS,)),
-            dma((CHUNKS,)),
-            dma((CHUNKS,)),
+            dma((CHUNKS, 2)),
+            dma((CHUNKS, 2)),
             dma((2, stages, CHUNKS)),
             dma((2, stages, CHUNKS)),
         ],

time: 77.5 us -> 73.6 us (0.950)
  Pallas kernels: 75.6 us -> 71.7 us
    pallas_call x1, Pallas kernels: 75.6 us -> 71.7 us  [by_halves(): pl.pallas_call(contraction, name='contraction', out_shape=jax.ShapeDtypeS...]
where the time goes in v3:
time: 73.6 us; the launch traced here: 73.5 us
  Pallas kernels  71.7 us (97%)
  local copies, waits for them, and re-layouts  1.73 us (2%)
    pallas_call x1, Pallas kernels, by_halves(): pl.pallas_call(contraction, name='contraction', out_shape=jax.ShapeDtypeS...  71.7 us
    reshape x2, local copies, waits for them, and re-layouts, by_halves(): return out.reshape(2, mine, 2, 2, lanes).transpose(1, 0, 2, 3, 4)  1.73 us

profile of v3, /device:TPU:0, one launch (start us, length us, event | category | flops | bytes accessed | tf_op | source)
XLA Modules:
  0.0 73.5 jit_solution(16762978400339199440)
XLA Ops:
  0.0 71.7 %contraction.1 = bf16[2,32,1024]{2,1,0:T(8,128)(2,1)} custom-call(s32[2,10]{1,0:T(2,128)} %order.1, s32[16]{0:T(128)} %pick.1, bf16[2,64,2,2,8,256]{5,4,3,2,1,0:T(8,128)(2,1)} %bitcast.5, bf16[2,1024,1024]{2,1,0:T(8,128)(2,1)} %b1.1, bf16[2,1024,1024]{2,1,0:T(8,128)(2,1)} %b2.1, bf16[2,2,16,32,512]{4,3,2,1,0:T(8,128)(2,1)} %bitcast.6), custom_call_target="tpu_custom_call" | custom-call | tf_op jit(solution)/shard_map/contraction/pallas_call | solution.py:525
  71.7 1.0 %reshape.11 = bf16[2,32,2,2,256]{4,3,2,1,0:T(2,128)(2,1)S(1)} reshape(bf16[2,32,1024]{2,1,0:T(8,128)(2,1)} %contraction.1) | data formatting | bytes 262144 | tf_op jit(solution)/shard_map/reshape | solution.py:565
  72.7 0.7 %copy.9 = bf16[2,32,2,2,256]{4,3,2,0,1:T(2,128)(2,1)} copy(bf16[2,32,2,2,256]{4,3,2,1,0:T(2,128)(2,1)S(1)} %reshape.11) | data formatting | bytes 262144 | tf_op jit(solution)/shard_map/reshape | solution.py:565

commit v4 on v3

--- a/solution.py
+++ b/solution.py
@@ -430,7 +430,7 @@
     swapped = widths[:1] + widths[1:-1][::-1] + widths[-1:]
 
     def order_of(u, k):
-        return widths
+        return swapped if u == 1 and k == CHUNKS - 1 else widths
 
     def exchange(u, stage, k):
         return pltpu.make_async_remote_copy(
@@ -461,9 +461,11 @@
             if stage < depth:
                 split(u, stage, k, total)
             else:
-                out[:, k * chunk : (k + 1) * chunk, u * columns : (u + 1) * columns] = total[
-                    :, 0
-                ].astype(out.dtype)
+                for r in range(2):
+                    for b in range(2):
+                        out[k * chunk : (k + 1) * chunk, r, u, b, :] = total[
+                            r, 0, :, b * lanes : (b + 1) * lanes
+                        ].astype(out.dtype)
 
     for step in range(CHUNKS + depth):
         if step < CHUNKS:
@@ -476,12 +478,12 @@
             for u in range(2):
                 part_of = total[:, u * columns : (u + 1) * columns]
                 split(u, 0, step, part_of.reshape(2, n, chunk, columns))
-            if ahead:
-                send_third(*ahead.pop(0))
-        for stage in range(depth, 0, -1):
+        for stage in range(1, depth + 1):
             k = step - stage + 1
             if 0 <= k < CHUNKS:
                 advance(stage, k)
+        if ahead:
+            send_third(*ahead.pop(0))
 
     @pl.when(inner)
     def _():
@@ -522,10 +524,10 @@
             for s in range(stages)
         ]
 
-    out = pl.pallas_call(
+    return pl.pallas_call(
         contraction,
         name="contraction",
-        out_shape=jax.ShapeDtypeStruct((2, mine, 4 * lanes), bf16),
+        out_shape=jax.ShapeDtypeStruct((mine, 2, 2, 2, lanes), bf16),
         in_specs=[smem, smem] + [anyspace] * 4,
         out_specs=pl.BlockSpec(memory_space=pltpu.VMEM),
         scratch_shapes=[
@@ -562,7 +564,6 @@
             collective_id=0, has_side_effects=True, vmem_limit_bytes=62 * 2**20
         ),
     )(leg_orders, slice_pick, cut, branch_one, branch_two, third)
-    return out.reshape(2, mine, 2, 2, lanes).transpose(1, 0, 2, 3, 4)
 
 
 def per_device(stem, branch_one, branch_two, branch_three, leg_orders, slice_pick):

time: 73.6 us -> 70.5 us (0.958)
  Pallas kernels: 71.7 us -> 68.6 us
    pallas_call x1, Pallas kernels: 71.7 us -> 68.6 us  [by_halves(): pl.pallas_call(contraction, name='contraction', out_shape=jax.ShapeDtypeS...]
    reshape x2 -> x0, local copies, waits for them, and re-layouts: 1.73 us -> none  [by_halves(): return out.reshape(2, mine, 2, 2, lanes).transpose(1, 0, 2, 3, 4)]
    unnamed x0 -> x1, local copies, waits for them, and re-layouts: none -> 1.65 us
where the time goes in v4:
time: 70.5 us; the launch traced here: 70.3 us
  Pallas kernels  68.6 us (97%)
  local copies, waits for them, and re-layouts  1.65 us (2%)
    pallas_call x1, Pallas kernels, by_halves(): pl.pallas_call(contraction, name='contraction', out_shape=jax.ShapeDtypeS...  68.6 us
    unnamed x1, local copies, waits for them, and re-layouts  1.65 us

profile of v4, /device:TPU:0, one launch (start us, length us, event | category | flops | bytes accessed | tf_op | source)
XLA Modules:
  0.0 70.3 jit_solution(16588833117977313449)
XLA Ops:
  0.0 68.6 %contraction.1 = bf16[32,2,2,2,256]{4,3,2,1,0:T(2,128)(2,1)} custom-call(s32[2,10]{1,0:T(2,128)} %order.1, s32[16]{0:T(128)} %pick.1, bf16[2,64,2,2,8,256]{5,4,3,2,1,0:T(8,128)(2,1)} %bitcast.2, bf16[2,1024,1024]{2,1,0:T(8,128)(2,1)} %b1.1, bf16[2,1024,1024]{2,1,0:T(8,128)(2,1)} %b2.1, bf16[2,2,16,32,512]{4,3,2,1,0:T(8,128)(2,1)} %bitcast.3), custom_call_target="tpu_custom_call" | custom-call | tf_op jit(solution)/shard_map/contraction/pallas_call | solution.py:527
  68.6 1.7 %copy.8 = bf16[32,2,2,2,256]{4,3,2,1,0:T(2,128)(2,1)} copy(bf16[32,2,2,2,256]{4,3,2,1,0:T(2,128)(2,1)} %contraction.1) | data formatting | bytes 262144

commit v5 on v4

--- a/solution.py
+++ b/solution.py
@@ -430,7 +430,7 @@
     swapped = widths[:1] + widths[1:-1][::-1] + widths[-1:]
 
     def order_of(u, k):
-        return swapped if u == 1 and k == CHUNKS - 1 else widths
+        return swapped if u == 1 and k >= CHUNKS - 2 else widths
 
     def exchange(u, stage, k):
         return pltpu.make_async_remote_copy(

time: 70.5 us -> 70.5 us (level)
  no operation moved by 1% of the time
where the time goes in v5:
time: 70.5 us; the launch traced here: 70.3 us
  Pallas kernels  68.7 us (97%)
  local copies, waits for them, and re-layouts  1.65 us (2%)
    pallas_call x1, Pallas kernels, by_halves(): pl.pallas_call(contraction, name='contraction', out_shape=jax.ShapeDtypeS...  68.7 us
    unnamed x1, local copies, waits for them, and re-layouts  1.65 us

profile of v5, /device:TPU:0, one launch (start us, length us, event | category | flops | bytes accessed | tf_op | source)
XLA Modules:
  0.0 70.3 jit_solution(232877289733286755)
XLA Ops:
  0.0 68.7 %contraction.1 = bf16[32,2,2,2,256]{4,3,2,1,0:T(2,128)(2,1)} custom-call(s32[2,10]{1,0:T(2,128)} %order.1, s32[16]{0:T(128)} %pick.1, bf16[2,64,2,2,8,256]{5,4,3,2,1,0:T(8,128)(2,1)} %bitcast.2, bf16[2,1024,1024]{2,1,0:T(8,128)(2,1)} %b1.1, bf16[2,1024,1024]{2,1,0:T(8,128)(2,1)} %b2.1, bf16[2,2,16,32,512]{4,3,2,1,0:T(8,128)(2,1)} %bitcast.3), custom_call_target="tpu_custom_call" | custom-call | tf_op jit(solution)/shard_map/contraction/pallas_call | solution.py:527
  68.7 1.7 %copy.8 = bf16[32,2,2,2,256]{4,3,2,1,0:T(2,128)(2,1)} copy(bf16[32,2,2,2,256]{4,3,2,1,0:T(2,128)(2,1)} %contraction.1) | data formatting | bytes 262144
